TPU v7x, 32 devices: a whole 2x2x4 slice. The times are simulated.
32 devices in a mesh: gz: 32 (over z, y, x, core).
Axes of the slice: x: 2, y: 2, z: 4, core: 2. Of those that a mesh axis runs over, the one named last changes fastest.
Arguments:
- velocity: float32 [3, 128, 256, 512], P(None, 'gz'), may hold values from -0.3 to 0.3
- offsets: float32 [3, 16384], P(None, 'gz'), may hold values from 1.2 to 1.8
- bases: int32 [3, 16384], P(None, 'gz'), may hold values from 0 to 511, as said below
- targets: float32 [3, 16384], P(None, 'gz'), may hold values from 1 to 2
- stiffness: float32 [16384], P('gz'), may hold values from 10 to 100
- active_block_count: int32 [32], P('gz'), may hold values from 1 to 2, as said below
Outputs:
- velocity_out: float32 [3, 128, 256, 512], P(None, 'gz')
- offsets_out: float32 [3, 16384], P(None, 'gz')
Inputs may be any that keep to these rules, and one draw needn't show every extreme that they name: `bases`: rows are x, y, z. x lies in 0..511 and y in 0..255; the z of marker m lies in the slab of index m // 512, from (m // 512) * 4 to (m // 512) * 4 + 3. `active_block_count`: in every draw some slab uses all 2 blocks.
All inputs are finite; a program needn't handle non-finite values.
Results may differ from a plain program's by a relative error of at most 0.0015.
Values may be sent and summed in bfloat16 or wider, within the bound.
A program may use at most 192 MiB of HBM per device.

v0:
```python
import functools
import math

import jax
import jax.numpy as jnp
from jax import lax
from jax.experimental import pallas as pl
from jax.experimental.pallas import tpu as pltpu
from jax.sharding import PartitionSpec as P

BLK = 256
STEPS = 2
DT = 0.2
VISC = 0.3
ROWS = 16


def shifted(value, steps):
    count = lax.axis_size("gz")
    pairs = [(source, (source + steps) % count) for source in range(count)]
    return lax.ppermute(value, "gz", pairs)


def joined(own_ref, near_ref, moved, layers):
    halves = []
    for ref, pair in ((own_ref, moved[:2]), (near_ref, moved[2:])):
        rows = ref[...]
        offsets = rows[0:3]
        if pair:
            sampled = pair[0][0:3, :] + pair[1][0:3, :]
            offsets = offsets + DT * (rows[9:10] * sampled)
        level = rows[5:6] if ref is own_ref else rows[5:6] - float(layers)
        forces = rows[10:11] * (rows[6:9] - offsets)
        halves.append((offsets, rows[3:5].astype(jnp.int32), level.astype(jnp.int32), forces))
    return [jnp.concatenate(parts, axis=1) for parts in zip(*halves)]


def weights_of(offsets):
    return [0.25 * (1.0 + jnp.cos((0.5 * math.pi) * (offsets - float(j)))) for j in range(4)]


def wrapped(cell, extent):
    return jnp.where(cell >= extent, cell - extent, cell)


def banded(across, cell, weights, extent):
    table = jnp.zeros(across.shape, jnp.float32)
    for j in range(4):
        table = jnp.where(across == wrapped(cell + j, extent), weights[j], table)
    return table


def plane_weights(level, weights_z, layers):
    planes = []
    for z in range(layers):
        row = jnp.zeros(level.shape, jnp.float32)
        for j in range(4):
            row = jnp.where(level + j == z, weights_z[j], row)
        planes.append(row)
    return planes


def columns_of(rows):
    pad = -len(rows) % 8
    zero = jnp.zeros_like(rows[0])
    return jnp.concatenate(rows + [zero] * pad, axis=0).T


def fill_xtable(table_ref, col_ref, first, low, extent, chunk):
    def body(i, _):
        r = pl.ds(i * chunk, chunk)
        cols = col_ref[r, :]
        across = lax.broadcasted_iota(jnp.int32, (chunk, extent), 1)
        cell = cols[:, first : first + 1].astype(jnp.int32)
        ws = [cols[:, first + 1 + j : first + 2 + j] for j in range(4)]
        table_ref[r, :] = banded(across, cell, ws, extent).astype(low)
        return 0

    lax.fori_loop(0, table_ref.shape[0] // chunk, body, 0)


def spread_kernel(layers, n_moved, *refs):
    own_ref, near_ref = refs[:2]
    moved = refs[2 : 2 + n_moved]
    v_hbm, p_hbm = refs[2 + n_moved : 4 + n_moved]
    vbuf, obuf, force, lhs, xtab, ytab, col, rowg, in_sem, out_sem = refs[4 + n_moved :]
    ny, nx = vbuf.shape[2], vbuf.shape[3]
    both = xtab.shape[0]

    load = pltpu.make_async_copy(v_hbm, vbuf, in_sem)
    load.start()

    offsets, cells, level, forces = joined(own_ref, near_ref, moved, layers)
    weights = weights_of(offsets)
    col[...] = columns_of(
        [cells[0:1].astype(jnp.float32)] + [w[0:1] for w in weights]
    )
    planes = plane_weights(level, [w[2:3] for w in weights], layers)
    for z in range(layers):
        rowg[z] = jnp.concatenate([forces * planes[z], jnp.zeros((5, both), jnp.float32)], axis=0)
    fill_xtable(xtab, col, 0, jnp.bfloat16, nx, 64)

    wy = [w[1:2] for w in weights]

    def ybody(i, _):
        across = lax.broadcasted_iota(jnp.int32, (8, both), 0) + i * 8
        ytab[pl.ds(i * 8, 8), :] = banded(across, cells[1:2], wy, ny)
        return 0

    lax.fori_loop(0, ny // 8, ybody, 0)
    load.wait()

    def plane(z, _):
        def lhs_body(i, _):
            y = ytab[pl.ds(i * 16, 16), :]
            for c in range(3):
                lhs[pl.ds(c * ny + i * 16, 16), :] = (rowg[z, c : c + 1, :] * y).astype(jnp.bfloat16)
            return 0

        lax.fori_loop(0, ny // 16, lhs_body, 0)
        force[...] = jnp.dot(lhs[...], xtab[...], preferred_element_type=jnp.float32)

        below = jnp.maximum(z - 1, 0)
        above = jnp.minimum(z + 1, layers - 1)
        has_below = jnp.where(z > 0, 1.0, 0.0)
        has_above = jnp.where(z < layers - 1, 1.0, 0.0)

        def stencil(i, _):
            n = 16
            y0 = i * n
            prev = jnp.where(i == 0, ny - 8, y0 - 8)
            nxt = jnp.where(y0 + n == ny, 0, y0 + n)
            here = [vbuf[c, z, pl.ds(y0, n), :] for c in range(3)]
            up = [DT * VISC - (0.5 * DT) * here[c] for c in range(3)]
            down = [DT * VISC + (0.5 * DT) * here[c] for c in range(3)]
            up[2] = up[2] * has_above
            down[2] = down[2] * has_below
            for c in range(3):
                window = jnp.concatenate(
                    [vbuf[c, z, pl.ds(prev, 8), :], here[c], vbuf[c, z, pl.ds(nxt, 8), :]], axis=0
                )
                total = (1.0 - 6.0 * DT * VISC) * here[c] + DT * force[pl.ds(c * ny + y0, n), :]
                total += up[0] * pltpu.roll(here[c], nx - 1, 1) + down[0] * pltpu.roll(here[c], 1, 1)
                total += up[1] * pltpu.roll(window, n + 15, 0)[8 : 8 + n]
                total += down[1] * pltpu.roll(window, 1, 0)[8 : 8 + n]
                total += up[2] * vbuf[c, above, pl.ds(y0, n), :]
                total += down[2] * vbuf[c, below, pl.ds(y0, n), :]
                obuf[c, z, pl.ds(y0, n), :] = total
            return 0

        lax.fori_loop(0, ny // 16, stencil, 0)
        pltpu.make_async_copy(obuf.at[:, z], p_hbm.at[:, z], out_sem.at[z]).start()
        return 0

    lax.fori_loop(0, layers, plane, 0)
    for z in range(layers):
        pltpu.make_async_copy(obuf.at[:, z], p_hbm.at[:, z], out_sem.at[z]).wait()


def spread_and_advance(own, near, moved, velocity):
    _, layers, ny, nx = velocity.shape
    both = 2 * own.shape[1]
    vmem = pl.BlockSpec(memory_space=pltpu.VMEM)
    hbm = pl.BlockSpec(memory_space=pl.ANY)
    flops = 2 * both * 3 * layers * ny * nx
    return pl.pallas_call(
        functools.partial(spread_kernel, layers, len(moved)),
        out_shape=jax.ShapeDtypeStruct(velocity.shape, jnp.float32),
        in_specs=[vmem] * (2 + len(moved)) + [hbm],
        out_specs=hbm,
        scratch_shapes=[
            pltpu.VMEM(velocity.shape, jnp.float32),
            pltpu.VMEM(velocity.shape, jnp.float32),
            pltpu.VMEM((3 * ny, nx), jnp.float32),
            pltpu.VMEM((3 * ny, both), jnp.bfloat16),
            pltpu.VMEM((both, nx), jnp.bfloat16),
            pltpu.VMEM((ny, both), jnp.float32),
            pltpu.VMEM((both, 8), jnp.float32),
            pltpu.VMEM((layers, 8, both), jnp.float32),
            pltpu.SemaphoreType.DMA,
            pltpu.SemaphoreType.DMA((layers,)),
        ],
        cost_estimate=pl.CostEstimate(
            flops=flops, bytes_accessed=8 * velocity.size, transcendentals=0
        ),
        name="spread_and_advance",
    )(own, near, *moved, velocity)


def edge_kernel(v_ref, p_ref, before_ref, after_ref, out_ref, *low_refs):
    side = pl.program_id(0)
    vz = v_ref[0, 0]

    @pl.when(side == 0)
    def _():
        down = DT * VISC + (0.5 * DT) * vz
        for c in range(3):
            new = p_ref[c, 0] + down * before_ref[c].astype(jnp.float32)
            out_ref[c, 0] = new
            if low_refs:
                low_refs[0][c] = new.astype(jnp.bfloat16)

    @pl.when(side == 1)
    def _():
        up = DT * VISC - (0.5 * DT) * vz
        for c in range(3):
            new = p_ref[c, 0] + up * after_ref[c].astype(jnp.float32)
            out_ref[c, 0] = new
            if low_refs:
                low_refs[1][c] = new.astype(jnp.bfloat16)


def finish_edges(velocity, partial, before, after, send):
    _, layers, ny, nx = velocity.shape
    yb = 64
    blocks = ny // yb
    wide = pl.BlockSpec((3, 1, yb, nx), lambda s, y: (0, s * (layers - 1), y, 0))
    head = pl.BlockSpec((3, yb, nx), lambda s, y: (0, jnp.where(s == 0, y, blocks - 1), 0))
    tail = pl.BlockSpec((3, yb, nx), lambda s, y: (0, jnp.where(s == 1, y, 0), 0))
    low = jax.ShapeDtypeStruct((3, ny, nx), jnp.bfloat16)
    return pl.pallas_call(
        edge_kernel,
        grid=(2, blocks),
        out_shape=[jax.ShapeDtypeStruct(partial.shape, jnp.float32)] + [low, low] * send,
        in_specs=[
            pl.BlockSpec((1, 1, yb, nx), lambda s, y: (2, s * (layers - 1), y, 0)),
            wide,
            head,
            tail,
        ],
        out_specs=[wide] + [head, tail] * send,
        input_output_aliases={1: 0},
        cost_estimate=pl.CostEstimate(
            flops=12 * ny * nx, bytes_accessed=50 * ny * nx, transcendentals=0
        ),
        name="finish_edges",
    )(velocity, partial, before, after)


def sample_kernel(layers, n_moved, *refs):
    own_ref, near_ref = refs[:2]
    moved = refs[2 : 2 + n_moved]
    v_hbm, own_out, near_out = refs[2 + n_moved : 5 + n_moved]
    vbuf, low, lhs, xtab, ytab, col, sem = refs[5 + n_moved :]
    ny, nx = vbuf.shape[2], vbuf.shape[3]
    both = xtab.shape[0]
    markers = both // 2

    copies = []
    for z in range(layers):
        copies.append(pltpu.make_async_copy(v_hbm.at[:, z], vbuf.at[:, z], sem.at[z]))
        copies[-1].start()

    offsets, cells, level, _ = joined(own_ref, near_ref, moved, layers)
    weights = weights_of(offsets)
    planes = plane_weights(level, [w[2:3] for w in weights], layers)
    rows = []
    for a in range(2):
        rows += [cells[a : a + 1].astype(jnp.float32)] + [w[a : a + 1] for w in weights]
    col[...] = columns_of(rows + planes)
    fill_xtable(xtab, col, 0, jnp.float32, nx, 64)
    fill_xtable(ytab, col, 5, jnp.float32, ny, 64)

    def lhs_body(i, _):
        r = pl.ds(i * 64, 64)
        y = ytab[r, :]
        cols = col[r, :]
        for z in range(layers):
            lhs[r, z * ny : (z + 1) * ny] = (cols[:, 10 + z : 11 + z] * y).astype(jnp.bfloat16)
        return 0

    lax.fori_loop(0, both // 64, lhs_body, 0)

    for z in range(layers):
        copies[z].wait()

        def low_body(i, _):
            r = pl.ds(i * 64, 64)
            for c in range(3):
                low[c, pl.ds(z * ny + i * 64, 64), :] = vbuf[c, z, r, :].astype(jnp.bfloat16)
            return 0

        lax.fori_loop(0, ny // 64, low_body, 0)

    for part, out, depth in ((0, own_out, layers * ny), (1, near_out, 3 * ny)):
        r = slice(part * markers, (part + 1) * markers)
        sums = []
        for c in range(3):
            lines = jnp.dot(
                lhs[r, :depth], low[c, :depth, :], preferred_element_type=jnp.float32
            )
            sums.append(jnp.sum(lines * xtab[r, :], axis=1, keepdims=True))
        zero = jnp.zeros((markers, 5), jnp.float32)
        out[...] = jnp.concatenate(sums + [zero], axis=1).T


def sample(own, near, moved, velocity):
    _, layers, ny, nx = velocity.shape
    markers = own.shape[1]
    both = 2 * markers
    vmem = pl.BlockSpec(memory_space=pltpu.VMEM)
    hbm = pl.BlockSpec(memory_space=pl.ANY)
    part = jax.ShapeDtypeStruct((8, markers), jnp.float32)
    return pl.pallas_call(
        functools.partial(sample_kernel, layers, len(moved)),
        out_shape=[part, part],
        in_specs=[vmem] * (2 + len(moved)) + [hbm],
        out_specs=[vmem, vmem],
        scratch_shapes=[
            pltpu.VMEM(velocity.shape, jnp.float32),
            pltpu.VMEM((3, layers * ny, nx), jnp.bfloat16),
            pltpu.VMEM((both, layers * ny), jnp.bfloat16),
            pltpu.VMEM((both, nx), jnp.float32),
            pltpu.VMEM((both, ny), jnp.float32),
            pltpu.VMEM((both, 16), jnp.float32),
            pltpu.SemaphoreType.DMA((layers,)),
        ],
        cost_estimate=pl.CostEstimate(
            flops=2 * both * 3 * layers * ny * nx,
            bytes_accessed=4 * velocity.size,
            transcendentals=0,
        ),
        name="sample",
    )(own, near, *moved, velocity)


def local(velocity, offsets, bases, targets, stiffness, active_block_count):
    layers = velocity.shape[1]
    markers = offsets.shape[1]
    living = (jnp.arange(markers, dtype=jnp.int32) // BLK < active_block_count[0]).astype(jnp.float32)
    level = bases[2] - lax.axis_index("gz") * layers
    own = jnp.concatenate(
        [
            offsets,
            bases[:2].astype(jnp.float32),
            level[None].astype(jnp.float32),
            targets,
            living[None],
            (living * stiffness)[None],
            jnp.zeros((ROWS - 11, markers), jnp.float32),
        ],
        axis=0,
    )
    near = shifted(own, 1)
    before = shifted(velocity[:, layers - 1].astype(jnp.bfloat16), 1)
    after = shifted(velocity[:, 0].astype(jnp.bfloat16), -1)
    moved = ()
    for step in range(STEPS):
        last = step == STEPS - 1
        partial = spread_and_advance(own, near, moved, velocity)
        done = finish_edges(velocity, partial, before, after, 0 if last else 1)
        velocity = done[0]
        if not last:
            before = shifted(done[2], 1)
            after = shifted(done[1], -1)
        own_part, near_part = sample(own, near, moved, velocity)
        back = shifted(near_part, -1)
        if not last:
            moved = (own_part, back, shifted(own_part, 1), near_part)
        offsets = offsets + DT * (living[None, :] * (own_part[:3] + back[:3]))
    return (velocity, offsets)


def solution(mesh):
    return jax.shard_map(
        local,
        mesh=mesh,
        in_specs=(
            P(None, "gz", None, None),
            P(None, "gz"),
            P(None, "gz"),
            P(None, "gz"),
            P("gz"),
            P("gz"),
        ),
        out_specs=(P(None, "gz", None, None), P(None, "gz")),
        check_vma=False,
    )
```

profile of v0, /device:TPU:0, one launch (start us, length us, event | category | flops | bytes accessed | tf_op | source)
XLA Modules:
  0.0 122.8 jit_solution(7293171414493319758)
XLA Ops:
  0.6 2.1 %slice_bitcast_fusion = (bf16[3,256,512]{2,1,0:T(8,128)(2,1)S(1)}, bf16[3,256,512]{2,1,0:T(8,128)(2,1)S(1)}) fusion(f32[3,4,256,512]{3,2,1,0:T(8,128)} %v_ref.1), kind=kLoop, calls=%fused_computation.1 | loop fusion | bytes 3145728 | tf_op jit(solution)/shard_map/convert_element_type | solution.py:346
  3.3 6.0 %collective-permute-start.2 = (bf16[3,256,512]{2,1,0:T(8,128)(2,1)S(1)}, bf16[3,256,512]{2,1,0:T(8,128)(2,1)S(1)}, u32[]{:S(2)}, u32[]{:S(2)}) collective-permute-start(bf16[3,256,512]{2,1,0:T(8,128)(2,1)S(1)} %get-tuple-element.16), channel_id=1, source_target_pairs={{0,31},{1,0},{2,1},{3,2},{4,3},{5,4},{6,5},{7,6},{8,7},{9,8},{10,9... | collective-permute-start | bytes 2359304 | tf_op jit(solution)/shard_map/ppermute | solution.py:21
  10.6 0.7 subtract_convert_fusion
  11.3 0.7 slice_convert_fusion
  12.0 1.5 %concatenate.3.refs_0_ = f32[16,512]{1,0:T(8,128)S(1)} concatenate(f32[3,512]{1,0:T(4,128)} %param.7, f32[2,512]{1,0:T(2,128)S(1)} %slice_convert_fusion, f32[1,512]{1,0:T(1,128)S(1)} %subtract_convert_fusion, f32[3,512]{1,0:T(4,128)} %param.9, f32[1,512]{1,0:T(1,128)S(1)} %compare_convert_fusion, f32[1,512]{1,0:T(1,128)S(1)} %bitcast.9, f32[5,512]{1,0:T(8,128)S(1)} %broadcast_in_dim.5), dimensions={0} | concatenate | bytes 65536 | tf_op jit(solution)/shard_map/concatenate | solution.py:332
  13.6 7.0 %collective-permute-done.refs_1_ = f32[16,512]{1,0:T(8,128)S(1)} collective-permute-done((f32[16,512]{1,0:T(8,128)S(1)}, f32[16,512]{1,0:T(8,128)S(1)}, u32[]{:S(2)}, u32[]{:S(2)}) %collective-permute-start) | collective-permute-done | bytes 32800 | tf_op jit(solution)/shard_map/ppermute | solution.py:21
  21.3 20.0 %spread_and_advance.2.p_ref = f32[3,4,256,512]{3,2,1,0:T(8,128)} custom-call(f32[16,512]{1,0:T(8,128)} %copy-done.4, f32[16,512]{1,0:T(8,128)} %copy-done.5, f32[3,4,256,512]{3,2,1,0:T(8,128)} %v_ref.1), custom_call_target="tpu_custom_call" | custom-call | flops 3221225472 | bytes 12582912 | tf_op jit(solution)/shard_map/spread_and_advance/pallas_call | solution.py:166
  41.3 0.9 copy-done.2
  42.2 0.9 copy-done.3
  43.1 7.3 %finish_edges.2 = (f32[3,4,256,512]{3,2,1,0:T(8,128)}, bf16[3,256,512]{2,1,0:T(8,128)(2,1)}, bf16[3,256,512]{2,1,0:T(8,128)(2,1)}) custom-call(f32[3,4,256,512]{3,2,1,0:T(8,128)} %v_ref.1, f32[3,4,256,512]{3,2,1,0:T(8,128)} %spread_and_advance.2.p_ref, bf16[3,256,512]{2,1,0:T(8,128)(2,1)} %copy-done.2, ...), custom_call_target="tpu_custom_call", output_to_operand_aliasing={{0}: (1, {})} | custom-call | flops 1572864 | bytes 6553600 | tf_op jit(solution)/shard_map/finish_edges/pallas_call | solution.py:221
  50.4 2.9 %collective-permute-start.5 = (bf16[3,256,512]{2,1,0:T(8,128)(2,1)}, bf16[3,256,512]{2,1,0:T(8,128)(2,1)S(1)}, u32[]{:S(2)}, u32[]{:S(2)}) collective-permute-start(bf16[3,256,512]{2,1,0:T(8,128)(2,1)} %get-tuple-element.12), channel_id=1, source_target_pairs={{0,1},{1,2},{2,3},{3,4},{4,5},{5,6},{6,7},{7,8},{8,9},{9,10},{10,1... | collective-permute-start | bytes 2359304 | tf_op jit(solution)/shard_map/ppermute | solution.py:21
  53.3 2.4 %collective-permute-start.6 = (bf16[3,256,512]{2,1,0:T(8,128)(2,1)}, bf16[3,256,512]{2,1,0:T(8,128)(2,1)S(1)}, u32[]{:S(2)}, u32[]{:S(2)}) collective-permute-start(bf16[3,256,512]{2,1,0:T(8,128)(2,1)} %get-tuple-element.13), channel_id=1, source_target_pairs={{0,31},{1,0},{2,1},{3,2},{4,3},{5,4},{6,5},{7,6},{8,7},{9,8},{10,9... | collective-permute-start | bytes 2359304 | tf_op jit(solution)/shard_map/ppermute | solution.py:21
  55.8 12.1 %sample.2 = (f32[8,512]{1,0:T(8,128)}, f32[8,512]{1,0:T(8,128)}) custom-call(f32[16,512]{1,0:T(8,128)} %copy-done.4, f32[16,512]{1,0:T(8,128)} %copy-done.5, f32[3,4,256,512]{3,2,1,0:T(8,128)} %get-tuple-element.9.refs_2_.refs_6_.v_ref), custom_call_target="tpu_custom_call" | custom-call | flops 3221225472 | bytes 6291456 | tf_op jit(solution)/shard_map/sample/pallas_call | solution.py:304
  67.8 2.8 %collective-permute-start.3 = (f32[8,512]{1,0:T(8,128)}, f32[8,512]{1,0:T(8,128)S(1)}, u32[]{:S(2)}, u32[]{:S(2)}) collective-permute-start(f32[8,512]{1,0:T(8,128)} %get-tuple-element.11.refs_5_), channel_id=1, source_target_pairs={{0,31},{1,0},{2,1},{3,2},{4,3},{5,4},{6,5},{7,6},{8,7},{9,8},{10,9... | collective-permute-start | bytes 49160 | tf_op jit(solution)/shard_map/ppermute | solution.py:21
  70.6 1.7 %collective-permute-done.3.refs_3_ = f32[8,512]{1,0:T(8,128)S(1)} collective-permute-done((f32[8,512]{1,0:T(8,128)}, f32[8,512]{1,0:T(8,128)S(1)}, u32[]{:S(2)}, u32[]{:S(2)}) %collective-permute-start.3) | collective-permute-done | bytes 16416 | tf_op jit(solution)/shard_map/ppermute | solution.py:21
  72.3 5.3 %collective-permute-done.4.refs_4_ = f32[8,512]{1,0:T(8,128)S(1)} collective-permute-done((f32[8,512]{1,0:T(8,128)}, f32[8,512]{1,0:T(8,128)S(1)}, u32[]{:S(2)}, u32[]{:S(2)}) %collective-permute-start.4) | collective-permute-done | bytes 16416 | tf_op jit(solution)/shard_map/ppermute | solution.py:21
  78.2 20.1 %spread_and_advance.3.p_ref = f32[3,4,256,512]{3,2,1,0:T(8,128)} custom-call(f32[16,512]{1,0:T(8,128)} %copy-done.4, f32[16,512]{1,0:T(8,128)} %copy-done.5, f32[8,512]{1,0:T(8,128)} %get-tuple-element.10.refs_2_, f32[8,512]{1,0:T(8,128)} %copy-done.7, f32[8,512]{1,0:T(8,128)} %copy-done.10, f32[8,512]{1,0:T(8,128)} %get-tuple-element.11.refs_5_, ...), custom_call_target="tpu_custom_call" | custom-call | flops 3221225472 | bytes 12582912 | tf_op jit(solution)/shard_map/spread_and_advance/pallas_call | solution.py:166
  98.3 0.9 copy-done
  99.2 0.9 copy-done.1
  100.1 6.7 %finish_edges.3.refs_6_ = f32[3,4,256,512]{3,2,1,0:T(8,128)} custom-call(f32[3,4,256,512]{3,2,1,0:T(8,128)} %get-tuple-element.9.refs_2_.refs_6_.v_ref, f32[3,4,256,512]{3,2,1,0:T(8,128)} %spread_and_advance.3.p_ref, bf16[3,256,512]{2,1,0:T(8,128)(2,1)} %copy-done, bf16[3,256,512]{2,1,0:T(8,128)(2,1)} %copy-done.1), custom_call_target="tpu_custom_call", output_to_operand_aliasing={{}: (1, {})} | custom-call | flops 1572864 | bytes 6553600 | tf_op jit(solution)/shard_map/finish_edges/pallas_call | solution.py:221
  106.9 12.2 %sample.3 = (f32[8,512]{1,0:T(8,128)}, f32[8,512]{1,0:T(8,128)}) custom-call(f32[16,512]{1,0:T(8,128)} %copy-done.4, f32[16,512]{1,0:T(8,128)} %copy-done.5, f32[8,512]{1,0:T(8,128)} %get-tuple-element.10.refs_2_, f32[8,512]{1,0:T(8,128)} %copy-done.7, f32[8,512]{1,0:T(8,128)} %copy-done.10, f32[8,512]{1,0:T(8,128)} %get-tuple-element.11.refs_5_, ...), custom_call_target="tpu_custom_call" | custom-call | flops 3221225472 | bytes 6291456 | tf_op jit(solution)/shard_map/sample/pallas_call | solution.py:304
  119.0 0.8 collective-permute-start.7
  119.8 1.6 %collective-permute-done.7 = f32[8,512]{1,0:T(8,128)S(1)} collective-permute-done((f32[8,512]{1,0:T(8,128)}, f32[8,512]{1,0:T(8,128)S(1)}, u32[]{:S(2)}, u32[]{:S(2)}) %collective-permute-start.7) | collective-permute-done | bytes 16416 | tf_op jit(solution)/shard_map/ppermute | solution.py:21
  121.4 1.3 %fusion.2 = f32[3,512]{1,0:T(4,128)} fusion(f32[8,512]{1,0:T(8,128)S(1)} %collective-permute-done.7, f32[3,512]{1,0:T(4,128)S(1)} %copy-done.9, f32[8,512]{1,0:T(8,128)S(1)} %copy-done.8, f32[8,512]{1,0:T(8,128)} %get-tuple-element.14, f32[8,512]{1,0:T(8,128)S(1)} %copy-done.6, f32[512]{0:T(512)S(1)} %fusion.10), kind=kLoop, calls=%fused_computation.6 | loop fusion | flops 12288 | bytes 38912 | tf_op jit(solution)/shard_map/add | solution.py:360
  (29 shorter events, 2.6 us)
Async XLA Ops:
  2.7 38.6 %collective-permute-start.1 = (bf16[3,256,512]{2,1,0:T(8,128)(2,1)S(1)}, bf16[3,256,512]{2,1,0:T(8,128)(2,1)S(1)}, u32[]{:S(2)}, u32[]{:S(2)}) collective-permute-start(bf16[3,256,512]{2,1,0:T(8,128)(2,1)S(1)} %get-tuple-element.17), channel_id=1, source_target_pairs={{0,1},{1,2},{2,3},{3,4},{4,5},{5,6},{6,7},{7,8},{8,9},{9,10},{10,1... | collective-permute-start | bytes 2359304 | tf_op jit(solution)/shard_map/ppermute | solution.py:21
  3.3 38.1 %collective-permute-start.2 = (bf16[3,256,512]{2,1,0:T(8,128)(2,1)S(1)}, bf16[3,256,512]{2,1,0:T(8,128)(2,1)S(1)}, u32[]{:S(2)}, u32[]{:S(2)}) collective-permute-start(bf16[3,256,512]{2,1,0:T(8,128)(2,1)S(1)} %get-tuple-element.16), channel_id=1, source_target_pairs={{0,31},{1,0},{2,1},{3,2},{4,3},{5,4},{6,5},{7,6},{8,7},{9,8},{10,9... | collective-permute-start | bytes 2359304 | tf_op jit(solution)/shard_map/ppermute | solution.py:21
  13.6 7.1 %copy-start.4 = (f32[16,512]{1,0:T(8,128)}, f32[16,512]{1,0:T(8,128)S(1)}, u32[]{:S(2)}) copy-start(f32[16,512]{1,0:T(8,128)S(1)} %concatenate.3.refs_0_) | copy-start | bytes 98308
  13.6 7.1 %collective-permute-start = (f32[16,512]{1,0:T(8,128)S(1)}, f32[16,512]{1,0:T(8,128)S(1)}, u32[]{:S(2)}, u32[]{:S(2)}) collective-permute-start(f32[16,512]{1,0:T(8,128)S(1)} %concatenate.3.refs_0_), channel_id=1, source_target_pairs={{0,1},{1,2},{2,3},{3,4},{4,5},{5,6},{6,7},{7,8},{8,9},{9,10},{10,1... | collective-permute-start | bytes 98312 | tf_op jit(solution)/shard_map/ppermute | solution.py:21
  20.6 0.6 copy-start.5
  41.3 0.9 copy-start.2
  42.2 0.9 copy-start.3
  50.4 47.9 %collective-permute-start.5 = (bf16[3,256,512]{2,1,0:T(8,128)(2,1)}, bf16[3,256,512]{2,1,0:T(8,128)(2,1)S(1)}, u32[]{:S(2)}, u32[]{:S(2)}) collective-permute-start(bf16[3,256,512]{2,1,0:T(8,128)(2,1)} %get-tuple-element.12), channel_id=1, source_target_pairs={{0,1},{1,2},{2,3},{3,4},{4,5},{5,6},{6,7},{7,8},{8,9},{9,10},{10,1... | collective-permute-start | bytes 2359304 | tf_op jit(solution)/shard_map/ppermute | solution.py:21
  53.3 45.0 %collective-permute-start.6 = (bf16[3,256,512]{2,1,0:T(8,128)(2,1)}, bf16[3,256,512]{2,1,0:T(8,128)(2,1)S(1)}, u32[]{:S(2)}, u32[]{:S(2)}) collective-permute-start(bf16[3,256,512]{2,1,0:T(8,128)(2,1)} %get-tuple-element.13), channel_id=1, source_target_pairs={{0,31},{1,0},{2,1},{3,2},{4,3},{5,4},{6,5},{7,6},{8,7},{9,8},{10,9... | collective-permute-start | bytes 2359304 | tf_op jit(solution)/shard_map/ppermute | solution.py:21
  67.8 4.4 %collective-permute-start.3 = (f32[8,512]{1,0:T(8,128)}, f32[8,512]{1,0:T(8,128)S(1)}, u32[]{:S(2)}, u32[]{:S(2)}) collective-permute-start(f32[8,512]{1,0:T(8,128)} %get-tuple-element.11.refs_5_), channel_id=1, source_target_pairs={{0,31},{1,0},{2,1},{3,2},{4,3},{5,4},{6,5},{7,6},{8,7},{9,8},{10,9... | collective-permute-start | bytes 49160 | tf_op jit(solution)/shard_map/ppermute | solution.py:21
  70.6 7.0 %collective-permute-start.4 = (f32[8,512]{1,0:T(8,128)}, f32[8,512]{1,0:T(8,128)S(1)}, u32[]{:S(2)}, u32[]{:S(2)}) collective-permute-start(f32[8,512]{1,0:T(8,128)} %get-tuple-element.10.refs_2_), channel_id=1, source_target_pairs={{0,1},{1,2},{2,3},{3,4},{4,5},{5,6},{6,7},{7,8},{8,9},{9,10},{10,1... | collective-permute-start | bytes 49160 | tf_op jit(solution)/shard_map/ppermute | solution.py:21
  72.3 5.3 %copy-start.7 = (f32[8,512]{1,0:T(8,128)}, f32[8,512]{1,0:T(8,128)S(1)}, u32[]{:S(2)}) copy-start(f32[8,512]{1,0:T(8,128)S(1)} %collective-permute-done.3.refs_3_) | copy-start | bytes 49156
  77.6 0.6 copy-start.10
  98.3 0.9 copy-start
  99.2 0.9 copy-start.1
  106.8 14.6 %copy-start.6 = (f32[8,512]{1,0:T(8,128)S(1)}, f32[8,512]{1,0:T(8,128)}, u32[]{:S(2)}) copy-start(f32[8,512]{1,0:T(8,128)} %get-tuple-element.10.refs_2_) | copy-start | bytes 49156
  106.8 14.6 %copy-start.8 = (f32[8,512]{1,0:T(8,128)S(1)}, f32[8,512]{1,0:T(8,128)}, u32[]{:S(2)}) copy-start(f32[8,512]{1,0:T(8,128)} %copy-done.7) | copy-start | bytes 49156
  106.8 14.6 %copy-start.9 = (f32[3,512]{1,0:T(4,128)S(1)}, f32[3,512]{1,0:T(4,128)}, u32[]{:S(2)}) copy-start(f32[3,512]{1,0:T(4,128)} %param.7) | copy-start | bytes 18436
  119.0 2.4 %collective-permute-start.7 = (f32[8,512]{1,0:T(8,128)}, f32[8,512]{1,0:T(8,128)S(1)}, u32[]{:S(2)}, u32[]{:S(2)}) collective-permute-start(f32[8,512]{1,0:T(8,128)} %get-tuple-element.15), channel_id=1, source_target_pairs={{0,31},{1,0},{2,1},{3,2},{4,3},{5,4},{6,5},{7,6},{8,7},{9,8},{10,9... | collective-permute-start | bytes 49160 | tf_op jit(solution)/shard_map/ppermute | solution.py:21
where the time goes:
time: 124 us; the launch traced here: 123 us
  Pallas kernels  78.4 us (63%)
  waiting for transfers between devices  15.6 us (13%)
  starting transfers between devices  15.4 us (12%)
  local copies, waits for them, and re-layouts  8.45 us (7%)
  other arithmetic  3.43 us (3%)
  between operations  1.41 us (1%)
    pallas_call x2, Pallas kernels, spread_and_advance(): pl.pallas_call(functools.partial(spread_kernel, layers, len(moved)), out_...  40.1 us
    pallas_call x2, Pallas kernels, sample(): pl.pallas_call(functools.partial(sample_kernel, layers, len(moved)), out_...  24.2 us
    ppermute x8, waiting for transfers between devices, shifted(): return lax.ppermute(value, 'gz', pairs)  15.6 us
    ppermute x8, starting transfers between devices, shifted(): return lax.ppermute(value, 'gz', pairs)  15.4 us
    pallas_call x2, Pallas kernels, finish_edges(): pl.pallas_call(edge_kernel, grid=(2, blocks), out_shape=[jax.ShapeDtypeSt...  14 us
    unnamed x22, local copies, waits for them, and re-layouts  4.81 us
  transfers between devices with their start and end apart: 8, of which 4 were waited for; matrix products, arithmetic and copies ran while one was open for 3% of the time, Pallas kernels for 43%

commit v1 on v0

--- a/solution.py
+++ b/solution.py
@@ -12,6 +12,7 @@
 STEPS = 2
 DT = 0.2
 VISC = 0.3
+TABLE = 128
 ROWS = 16
 
 
@@ -36,17 +37,20 @@
 
 
 def weights_of(offsets):
-    return [0.25 * (1.0 + jnp.cos((0.5 * math.pi) * (offsets - float(j)))) for j in range(4)]
-
-
-def wrapped(cell, extent):
-    return jnp.where(cell >= extent, cell - extent, cell)
+    angle = (0.5 * math.pi) * offsets
+    c, s = jnp.cos(angle), jnp.sin(angle)
+    return [0.25 * (1.0 + c), 0.25 * (1.0 + s), 0.25 * (1.0 - c), 0.25 * (1.0 - s)]
 
 
 def banded(across, cell, weights, extent):
-    table = jnp.zeros(across.shape, jnp.float32)
-    for j in range(4):
-        table = jnp.where(across == wrapped(cell + j, extent), weights[j], table)
+    apart = across - cell
+    if extent & (extent - 1) == 0:
+        apart = apart & (extent - 1)
+    else:
+        apart = jnp.where(apart < 0, apart + extent, apart)
+    table = jnp.where(apart == 3, weights[3], 0.0)
+    for j in (2, 1, 0):
+        table = jnp.where(apart == j, weights[j], table)
     return table
 
 
@@ -82,8 +86,8 @@
 def spread_kernel(layers, n_moved, *refs):
     own_ref, near_ref = refs[:2]
     moved = refs[2 : 2 + n_moved]
-    v_hbm, p_hbm = refs[2 + n_moved : 4 + n_moved]
-    vbuf, obuf, force, lhs, xtab, ytab, col, rowg, in_sem, out_sem = refs[4 + n_moved :]
+    v_hbm, p_hbm, col = refs[2 + n_moved : 5 + n_moved]
+    vbuf, obuf, force, lhs, xtab, ytab, rowg, in_sem, out_sem = refs[5 + n_moved :]
     ny, nx = vbuf.shape[2], vbuf.shape[3]
     both = xtab.shape[0]
 
@@ -92,22 +96,23 @@
 
     offsets, cells, level, forces = joined(own_ref, near_ref, moved, layers)
     weights = weights_of(offsets)
-    col[...] = columns_of(
-        [cells[0:1].astype(jnp.float32)] + [w[0:1] for w in weights]
-    )
     planes = plane_weights(level, [w[2:3] for w in weights], layers)
+    rows = []
+    for a in range(2):
+        rows += [cells[a : a + 1].astype(jnp.float32)] + [w[a : a + 1] for w in weights]
+    col[...] = columns_of(rows + planes)
     for z in range(layers):
         rowg[z] = jnp.concatenate([forces * planes[z], jnp.zeros((5, both), jnp.float32)], axis=0)
-    fill_xtable(xtab, col, 0, jnp.bfloat16, nx, 64)
+    fill_xtable(xtab, col, 0, jnp.bfloat16, nx, TABLE)
 
     wy = [w[1:2] for w in weights]
 
     def ybody(i, _):
-        across = lax.broadcasted_iota(jnp.int32, (8, both), 0) + i * 8
-        ytab[pl.ds(i * 8, 8), :] = banded(across, cells[1:2], wy, ny)
-        return 0
-
-    lax.fori_loop(0, ny // 8, ybody, 0)
+        across = lax.broadcasted_iota(jnp.int32, (32, both), 0) + i * 32
+        ytab[pl.ds(i * 32, 32), :] = banded(across, cells[1:2], wy, ny)
+        return 0
+
+    lax.fori_loop(0, ny // 32, ybody, 0)
     load.wait()
 
     def plane(z, _):
@@ -165,9 +170,12 @@
     flops = 2 * both * 3 * layers * ny * nx
     return pl.pallas_call(
         functools.partial(spread_kernel, layers, len(moved)),
-        out_shape=jax.ShapeDtypeStruct(velocity.shape, jnp.float32),
+        out_shape=[
+            jax.ShapeDtypeStruct(velocity.shape, jnp.float32),
+            jax.ShapeDtypeStruct((both, 16), jnp.float32),
+        ],
         in_specs=[vmem] * (2 + len(moved)) + [hbm],
-        out_specs=hbm,
+        out_specs=[hbm, vmem],
         scratch_shapes=[
             pltpu.VMEM(velocity.shape, jnp.float32),
             pltpu.VMEM(velocity.shape, jnp.float32),
@@ -175,7 +183,6 @@
             pltpu.VMEM((3 * ny, both), jnp.bfloat16),
             pltpu.VMEM((both, nx), jnp.bfloat16),
             pltpu.VMEM((ny, both), jnp.float32),
-            pltpu.VMEM((both, 8), jnp.float32),
             pltpu.VMEM((layers, 8, both), jnp.float32),
             pltpu.SemaphoreType.DMA,
             pltpu.SemaphoreType.DMA((layers,)),
@@ -187,100 +194,72 @@
     )(own, near, *moved, velocity)
 
 
-def edge_kernel(v_ref, p_ref, before_ref, after_ref, out_ref, *low_refs):
-    side = pl.program_id(0)
-    vz = v_ref[0, 0]
-
-    @pl.when(side == 0)
-    def _():
-        down = DT * VISC + (0.5 * DT) * vz
-        for c in range(3):
-            new = p_ref[c, 0] + down * before_ref[c].astype(jnp.float32)
-            out_ref[c, 0] = new
-            if low_refs:
-                low_refs[0][c] = new.astype(jnp.bfloat16)
-
-    @pl.when(side == 1)
-    def _():
-        up = DT * VISC - (0.5 * DT) * vz
-        for c in range(3):
-            new = p_ref[c, 0] + up * after_ref[c].astype(jnp.float32)
-            out_ref[c, 0] = new
-            if low_refs:
-                low_refs[1][c] = new.astype(jnp.bfloat16)
-
-
-def finish_edges(velocity, partial, before, after, send):
-    _, layers, ny, nx = velocity.shape
-    yb = 64
-    blocks = ny // yb
-    wide = pl.BlockSpec((3, 1, yb, nx), lambda s, y: (0, s * (layers - 1), y, 0))
-    head = pl.BlockSpec((3, yb, nx), lambda s, y: (0, jnp.where(s == 0, y, blocks - 1), 0))
-    tail = pl.BlockSpec((3, yb, nx), lambda s, y: (0, jnp.where(s == 1, y, 0), 0))
-    low = jax.ShapeDtypeStruct((3, ny, nx), jnp.bfloat16)
-    return pl.pallas_call(
-        edge_kernel,
-        grid=(2, blocks),
-        out_shape=[jax.ShapeDtypeStruct(partial.shape, jnp.float32)] + [low, low] * send,
-        in_specs=[
-            pl.BlockSpec((1, 1, yb, nx), lambda s, y: (2, s * (layers - 1), y, 0)),
-            wide,
-            head,
-            tail,
-        ],
-        out_specs=[wide] + [head, tail] * send,
-        input_output_aliases={1: 0},
-        cost_estimate=pl.CostEstimate(
-            flops=12 * ny * nx, bytes_accessed=50 * ny * nx, transcendentals=0
-        ),
-        name="finish_edges",
-    )(velocity, partial, before, after)
-
-
-def sample_kernel(layers, n_moved, *refs):
-    own_ref, near_ref = refs[:2]
-    moved = refs[2 : 2 + n_moved]
-    v_hbm, own_out, near_out = refs[2 + n_moved : 5 + n_moved]
-    vbuf, low, lhs, xtab, ytab, col, sem = refs[5 + n_moved :]
+def sample_kernel(layers, send, *refs):
+    col, v_hbm, p_hbm, before_hbm, after_hbm, out_hbm, own_out, near_out = refs[:8]
+    low_hbm = refs[8 : 8 + 2 * send]
+    vbuf, vz, halo, low, lhs, xtab, sem, out_sem = refs[8 + 2 * send :]
     ny, nx = vbuf.shape[2], vbuf.shape[3]
     both = xtab.shape[0]
     markers = both // 2
-
-    copies = []
-    for z in range(layers):
-        copies.append(pltpu.make_async_copy(v_hbm.at[:, z], vbuf.at[:, z], sem.at[z]))
-        copies[-1].start()
-
-    offsets, cells, level, _ = joined(own_ref, near_ref, moved, layers)
-    weights = weights_of(offsets)
-    planes = plane_weights(level, [w[2:3] for w in weights], layers)
-    rows = []
-    for a in range(2):
-        rows += [cells[a : a + 1].astype(jnp.float32)] + [w[a : a + 1] for w in weights]
-    col[...] = columns_of(rows + planes)
-    fill_xtable(xtab, col, 0, jnp.float32, nx, 64)
-    fill_xtable(ytab, col, 5, jnp.float32, ny, 64)
+    edges = ((0, before_hbm, 0.5 * DT), (layers - 1, after_hbm, -0.5 * DT))
+
+    loads = []
+    for side, (z, halo_hbm, _) in enumerate(edges):
+        loads.append(pltpu.make_async_copy(p_hbm.at[:, z], vbuf.at[:, z], sem.at[z]))
+        loads.append(pltpu.make_async_copy(v_hbm.at[2, z], vz.at[side], sem.at[layers + side]))
+        loads.append(pltpu.make_async_copy(halo_hbm, halo.at[side], sem.at[layers + 2 + side]))
+    for z in range(1, layers - 1):
+        loads.append(pltpu.make_async_copy(p_hbm.at[:, z], vbuf.at[:, z], sem.at[z]))
+    for load in loads:
+        load.start()
+
+    fill_xtable(xtab, col, 0, jnp.float32, nx, TABLE)
 
     def lhs_body(i, _):
-        r = pl.ds(i * 64, 64)
-        y = ytab[r, :]
+        r = pl.ds(i * TABLE, TABLE)
         cols = col[r, :]
+        across = lax.broadcasted_iota(jnp.int32, (TABLE, ny), 1)
+        cell = cols[:, 5:6].astype(jnp.int32)
+        y = banded(across, cell, [cols[:, 6 + j : 7 + j] for j in range(4)], ny)
         for z in range(layers):
             lhs[r, z * ny : (z + 1) * ny] = (cols[:, 10 + z : 11 + z] * y).astype(jnp.bfloat16)
         return 0
 
-    lax.fori_loop(0, both // 64, lhs_body, 0)
-
-    for z in range(layers):
-        copies[z].wait()
-
-        def low_body(i, _):
-            r = pl.ds(i * 64, 64)
+    lax.fori_loop(0, both // TABLE, lhs_body, 0)
+    for load in loads:
+        load.wait()
+
+    stores = []
+    for side, (z, _, sign) in enumerate(edges):
+
+        def edge_body(i, _):
+            r = pl.ds(i * 32, 32)
+            factor = DT * VISC + sign * vz[side, r, :]
             for c in range(3):
-                low[c, pl.ds(z * ny + i * 64, 64), :] = vbuf[c, z, r, :].astype(jnp.bfloat16)
+                new = vbuf[c, z, r, :] + factor * halo[side, c, r, :].astype(jnp.float32)
+                vbuf[c, z, r, :] = new
+                low[c, pl.ds(z * ny + i * 32, 32), :] = new.astype(jnp.bfloat16)
             return 0
 
-        lax.fori_loop(0, ny // 64, low_body, 0)
+        lax.fori_loop(0, ny // 32, edge_body, 0)
+        stores.append(pltpu.make_async_copy(vbuf.at[:, z], out_hbm.at[:, z], out_sem.at[side]))
+        if send:
+            stores.append(
+                pltpu.make_async_copy(
+                    low.at[:, z * ny : (z + 1) * ny], low_hbm[side], out_sem.at[2 + side]
+                )
+            )
+    for store in stores:
+        store.start()
+
+    def low_body(i, _):
+        r = pl.ds(i * 32, 32)
+        for z in range(1, layers - 1):
+            for c in range(3):
+                low[c, pl.ds(z * ny + i * 32, 32), :] = vbuf[c, z, r, :].astype(jnp.bfloat16)
+        return 0
+
+    lax.fori_loop(0, ny // 32, low_body, 0)
 
     for part, out, depth in ((0, own_out, layers * ny), (1, near_out, 3 * ny)):
         r = slice(part * markers, (part + 1) * markers)
@@ -292,36 +271,41 @@
             sums.append(jnp.sum(lines * xtab[r, :], axis=1, keepdims=True))
         zero = jnp.zeros((markers, 5), jnp.float32)
         out[...] = jnp.concatenate(sums + [zero], axis=1).T
-
-
-def sample(own, near, moved, velocity):
+    for store in stores:
+        store.wait()
+
+
+def finish_and_sample(col, velocity, partial, before, after, send):
     _, layers, ny, nx = velocity.shape
-    markers = own.shape[1]
-    both = 2 * markers
+    both = col.shape[0]
+    markers = both // 2
     vmem = pl.BlockSpec(memory_space=pltpu.VMEM)
     hbm = pl.BlockSpec(memory_space=pl.ANY)
     part = jax.ShapeDtypeStruct((8, markers), jnp.float32)
+    low = jax.ShapeDtypeStruct((3, ny, nx), jnp.bfloat16)
     return pl.pallas_call(
-        functools.partial(sample_kernel, layers, len(moved)),
-        out_shape=[part, part],
-        in_specs=[vmem] * (2 + len(moved)) + [hbm],
-        out_specs=[vmem, vmem],
+        functools.partial(sample_kernel, layers, send),
+        out_shape=[jax.ShapeDtypeStruct(velocity.shape, jnp.float32), part, part] + [low, low] * send,
+        in_specs=[vmem] + [hbm] * 4,
+        out_specs=[hbm, vmem, vmem] + [hbm, hbm] * send,
+        input_output_aliases={2: 0},
         scratch_shapes=[
             pltpu.VMEM(velocity.shape, jnp.float32),
+            pltpu.VMEM((2, ny, nx), jnp.float32),
+            pltpu.VMEM((2, 3, ny, nx), jnp.bfloat16),
             pltpu.VMEM((3, layers * ny, nx), jnp.bfloat16),
             pltpu.VMEM((both, layers * ny), jnp.bfloat16),
             pltpu.VMEM((both, nx), jnp.float32),
-            pltpu.VMEM((both, ny), jnp.float32),
-            pltpu.VMEM((both, 16), jnp.float32),
-            pltpu.SemaphoreType.DMA((layers,)),
+            pltpu.SemaphoreType.DMA((layers + 4,)),
+            pltpu.SemaphoreType.DMA((4,)),
         ],
         cost_estimate=pl.CostEstimate(
             flops=2 * both * 3 * layers * ny * nx,
             bytes_accessed=4 * velocity.size,
             transcendentals=0,
         ),
-        name="sample",
-    )(own, near, *moved, velocity)
+        name="finish_and_sample",
+    )(col, velocity, partial, before, after)
 
 
 def local(velocity, offsets, bases, targets, stiffness, active_block_count):
@@ -341,21 +325,25 @@
         ],
         axis=0,
     )
+    first = velocity[:, 0].astype(jnp.bfloat16)
+    final = velocity[:, layers - 1].astype(jnp.bfloat16)
     near = shifted(own, 1)
-    before = shifted(velocity[:, layers - 1].astype(jnp.bfloat16), 1)
-    after = shifted(velocity[:, 0].astype(jnp.bfloat16), -1)
     moved = ()
     for step in range(STEPS):
         last = step == STEPS - 1
-        partial = spread_and_advance(own, near, moved, velocity)
-        done = finish_edges(velocity, partial, before, after, 0 if last else 1)
-        velocity = done[0]
-        if not last:
-            before = shifted(done[2], 1)
-            after = shifted(done[1], -1)
-        own_part, near_part = sample(own, near, moved, velocity)
+        if moved:
+            first, final, *moved = lax.optimization_barrier((first, final, *moved))
+        else:
+            first, final, near = lax.optimization_barrier((first, final, near))
+        before = shifted(final, 1)
+        after = shifted(first, -1)
+        partial, col = spread_and_advance(own, near, moved, velocity)
+        velocity, own_part, near_part, *low = finish_and_sample(
+            col, velocity, partial, before, after, 0 if last else 1
+        )
         back = shifted(near_part, -1)
         if not last:
+            first, final = low
             moved = (own_part, back, shifted(own_part, 1), near_part)
         offsets = offsets + DT * (living[None, :] * (own_part[:3] + back[:3]))
     return (velocity, offsets)

time: 124 us -> 94.7 us (0.76)
  Pallas kernels: 78.4 us -> 57.6 us
  starting transfers between devices: 15.4 us -> 11.8 us
  local copies, waits for them, and re-layouts: 8.45 us -> 5.98 us
  waiting for transfers between devices: 15.6 us -> 13.7 us
    pallas_call x4 -> x2, Pallas kernels: 38.3 us -> 18.5 us  [finish_and_sample(): pl.pallas_call(functools.partial(sample_kernel, layers, send), out_shape=...]
    ppermute x8, starting transfers between devices: 15.4 us -> 11.8 us  [shifted(): return lax.ppermute(value, 'gz', pairs)]
    unnamed x22, local copies, waits for them, and re-layouts: 4.81 us -> 2.35 us
    ppermute x8, waiting for transfers between devices: 15.6 us -> 13.7 us  [shifted(): return lax.ppermute(value, 'gz', pairs)]
  transfers between devices with their start and end apart: 8 -> 8, of which waited for: 4 -> 4; matrix products, arithmetic and copies ran while one was open for 3% -> 2% of each run, Pallas kernels for 43% -> 42%
where the time goes in v1:
time: 94.7 us; the launch traced here: 94 us
  Pallas kernels  57.6 us (61%)
  waiting for transfers between devices  13.7 us (14%)
  starting transfers between devices  11.8 us (12%)
  local copies, waits for them, and re-layouts  5.98 us (6%)
  other arithmetic  3.43 us (4%)
  between operations  1.42 us (1%)
    pallas_call x2, Pallas kernels, spread_and_advance(): pl.pallas_call(functools.partial(spread_kernel, layers, len(moved)), out_...  39.1 us
    pallas_call x2, Pallas kernels, finish_and_sample(): pl.pallas_call(functools.partial(sample_kernel, layers, send), out_shape=...  18.5 us
    ppermute x8, waiting for transfers between devices, shifted(): return lax.ppermute(value, 'gz', pairs)  13.7 us
    ppermute x8, starting transfers between devices, shifted(): return lax.ppermute(value, 'gz', pairs)  11.8 us
    unnamed x22, local copies, waits for them, and re-layouts  2.35 us
    convert_element_type x1, local copies, waits for them, and re-layouts, local(): final = velocity[:, layers - 1].astype(jnp.bfloat16)  2.08 us
  transfers between devices with their start and end apart: 8, of which 4 were waited for; matrix products, arithmetic and copies ran while one was open for 2% of the time, Pallas kernels for 42%

profile of v1, /device:TPU:0, one launch (start us, length us, event | category | flops | bytes accessed | tf_op | source)
XLA Modules:
  0.0 94.0 jit_solution(6818368182303774501)
XLA Ops:
  1.3 0.7 slice_convert_fusion
  2.0 0.7 subtract_convert_fusion
  2.7 0.7 broadcast_select_fusion
  3.4 1.5 %concatenate.3.refs_0_ = f32[16,512]{1,0:T(8,128)S(1)} concatenate(f32[3,512]{1,0:T(4,128)} %param.7, f32[2,512]{1,0:T(2,128)S(1)} %slice_convert_fusion, f32[1,512]{1,0:T(1,128)S(1)} %subtract_convert_fusion, f32[3,512]{1,0:T(4,128)} %param.9, f32[1,512]{1,0:T(1,128)S(1)} %compare_convert_fusion, f32[1,512]{1,0:T(1,128)S(1)} %bitcast.9, f32[5,512]{1,0:T(8,128)S(1)} %broadcast_in_dim.5), dimensions={0} | concatenate | bytes 65536 | tf_op jit(solution)/shard_map/concatenate | solution.py:316
  4.9 0.5 collective-permute-start
  5.5 2.1 %slice_bitcast_fusion = (bf16[3,256,512]{2,1,0:T(8,128)(2,1)S(1)}, bf16[3,256,512]{2,1,0:T(8,128)(2,1)S(1)}) fusion(f32[3,4,256,512]{3,2,1,0:T(8,128)} %refs_1_.1), kind=kLoop, calls=%fused_computation.1 | loop fusion | bytes 3145728 | tf_op jit(solution)/shard_map/convert_element_type | solution.py:329
  7.6 5.4 %collective-permute-done.refs_1_ = f32[16,512]{1,0:T(8,128)S(1)} collective-permute-done((f32[16,512]{1,0:T(8,128)S(1)}, f32[16,512]{1,0:T(8,128)S(1)}, u32[]{:S(2)}, u32[]{:S(2)}) %collective-permute-start) | collective-permute-done | bytes 32800 | tf_op jit(solution)/shard_map/ppermute | solution.py:22
  13.0 5.3 %collective-permute-start.2 = (bf16[3,256,512]{2,1,0:T(8,128)(2,1)S(1)}, bf16[3,256,512]{2,1,0:T(8,128)(2,1)S(1)}, u32[]{:S(2)}, u32[]{:S(2)}) collective-permute-start(bf16[3,256,512]{2,1,0:T(8,128)(2,1)S(1)} %get-tuple-element.27), channel_id=1, source_target_pairs={{0,31},{1,0},{2,1},{3,2},{4,3},{5,4},{6,5},{7,6},{8,7},{9,8},{10,9... | collective-permute-start | bytes 2359304 | tf_op jit(solution)/shard_map/ppermute | solution.py:22
  18.3 19.5 %spread_and_advance.2 = (f32[3,4,256,512]{3,2,1,0:T(8,128)}, f32[1024,16]{1,0:T(8,128)}) custom-call(f32[16,512]{1,0:T(8,128)} %copy-done.5, f32[16,512]{1,0:T(8,128)} %copy-done.9, f32[3,4,256,512]{3,2,1,0:T(8,128)} %refs_1_.1), custom_call_target="tpu_custom_call" | custom-call | flops 3221225472 | bytes 12582912 | tf_op jit(solution)/shard_map/spread_and_advance/pallas_call | solution.py:171
  37.9 0.8 copy-done.2
  38.8 0.3 copy-done.3
  39.1 9.2 %finish_and_sample.2 = (f32[3,4,256,512]{3,2,1,0:T(8,128)}, f32[8,512]{1,0:T(8,128)}, f32[8,512]{1,0:T(8,128)}, bf16[3,256,512]{2,1,0:T(8,128)(2,1)}, bf16[3,256,512]{2,1,0:T(8,128)(2,1)}) custom-call(f32[1024,16]{1,0:T(8,128)} %get-tuple-element.24.refs_0_, f32[3,4,256,512]{3,2,1,0:T(8,128)} %refs_1_.1, ...), custom_call_target="tpu_custom_call", output_to_operand_aliasing={{0}: (2, {})} | custom-call | flops 3221225472 | bytes 6291456 | tf_op jit(solution)/shard_map/finish_and_sample/pallas_call | solution.py:286
  48.4 0.1 collective-permute-start.3
  48.4 0.5 collective-permute-start.4
  48.9 1.2 %collective-permute-done.3.refs_3_ = f32[8,512]{1,0:T(8,128)S(1)} collective-permute-done((f32[8,512]{1,0:T(8,128)}, f32[8,512]{1,0:T(8,128)S(1)}, u32[]{:S(2)}, u32[]{:S(2)}) %collective-permute-start.3) | collective-permute-done | bytes 16416 | tf_op jit(solution)/shard_map/ppermute | solution.py:22
  50.1 5.5 %collective-permute-done.4.refs_4_ = f32[8,512]{1,0:T(8,128)S(1)} collective-permute-done((f32[8,512]{1,0:T(8,128)}, f32[8,512]{1,0:T(8,128)S(1)}, u32[]{:S(2)}, u32[]{:S(2)}) %collective-permute-start.4) | collective-permute-done | bytes 16416 | tf_op jit(solution)/shard_map/ppermute | solution.py:22
  55.5 5.3 %collective-permute-start.6 = (bf16[3,256,512]{2,1,0:T(8,128)(2,1)}, bf16[3,256,512]{2,1,0:T(8,128)(2,1)S(1)}, u32[]{:S(2)}, u32[]{:S(2)}) collective-permute-start(bf16[3,256,512]{2,1,0:T(8,128)(2,1)} %get-tuple-element.40), channel_id=1, source_target_pairs={{0,31},{1,0},{2,1},{3,2},{4,3},{5,4},{6,5},{7,6},{8,7},{9,8},{10,9... | collective-permute-start | bytes 2359304 | tf_op jit(solution)/shard_map/ppermute | solution.py:22
  60.9 19.6 %spread_and_advance.3 = (f32[3,4,256,512]{3,2,1,0:T(8,128)}, f32[1024,16]{1,0:T(8,128)}) custom-call(f32[16,512]{1,0:T(8,128)} %copy-done.5, f32[16,512]{1,0:T(8,128)} %copy-done.9, f32[8,512]{1,0:T(8,128)} %get-tuple-element.32.refs_2_, f32[8,512]{1,0:T(8,128)} %copy-done.7, f32[8,512]{1,0:T(8,128)} %copy-done.10, f32[8,512]{1,0:T(8,128)} %get-tuple-element.35.refs_5_, ...), custom_call_target="tpu_custom_call" | custom-call | flops 3221225472 | bytes 12582912 | tf_op jit(solution)/shard_map/spread_and_advance/pallas_call | solution.py:171
  80.5 0.9 copy-done
  81.4 0.3 copy-done.1
  81.6 9.3 %finish_and_sample.3 = (f32[3,4,256,512]{3,2,1,0:T(8,128)}, f32[8,512]{1,0:T(8,128)}, f32[8,512]{1,0:T(8,128)}) custom-call(f32[1024,16]{1,0:T(8,128)} %get-tuple-element.37.refs_0_, f32[3,4,256,512]{3,2,1,0:T(8,128)} %get-tuple-element.36.refs_6_.refs_1_, f32[3,4,256,512]{3,2,1,0:T(8,128)} %get-tuple-element.38.refs_2_, ...), custom_call_target="tpu_custom_call", output_to_operand_aliasing={{0}: (2, {})} | custom-call | flops 3221225472 | bytes 6291456 | tf_op jit(solution)/shard_map/finish_and_sample/pallas_call | solution.py:286
  90.9 0.1 collective-permute-start.7
  91.0 1.6 %collective-permute-done.7 = f32[8,512]{1,0:T(8,128)S(1)} collective-permute-done((f32[8,512]{1,0:T(8,128)}, f32[8,512]{1,0:T(8,128)S(1)}, u32[]{:S(2)}, u32[]{:S(2)}) %collective-permute-start.7) | collective-permute-done | bytes 16416 | tf_op jit(solution)/shard_map/ppermute | solution.py:22
  92.7 1.3 %fusion.2 = f32[3,512]{1,0:T(4,128)} fusion(f32[8,512]{1,0:T(8,128)S(1)} %collective-permute-done.7, f32[3,512]{1,0:T(4,128)S(1)} %copy-done.4, f32[8,512]{1,0:T(8,128)S(1)} %copy-done.8, f32[8,512]{1,0:T(8,128)} %get-tuple-element.42, f32[8,512]{1,0:T(8,128)S(1)} %copy-done.6, f32[512]{0:T(512)S(1)} %fusion.10), kind=kLoop, calls=%fused_computation.6 | loop fusion | flops 12288 | bytes 38912 | tf_op jit(solution)/shard_map/add | solution.py:348
  (27 shorter events, 0.1 us)
Async XLA Ops:
  4.9 13.4 %copy-start.5 = (f32[16,512]{1,0:T(8,128)}, f32[16,512]{1,0:T(8,128)S(1)}, u32[]{:S(2)}) copy-start(f32[16,512]{1,0:T(8,128)S(1)} %concatenate.3.refs_0_) | copy-start | bytes 98308
  4.9 8.1 %collective-permute-start = (f32[16,512]{1,0:T(8,128)S(1)}, f32[16,512]{1,0:T(8,128)S(1)}, u32[]{:S(2)}, u32[]{:S(2)}) collective-permute-start(f32[16,512]{1,0:T(8,128)S(1)} %concatenate.3.refs_0_), channel_id=1, source_target_pairs={{0,1},{1,2},{2,3},{3,4},{4,5},{5,6},{6,7},{7,8},{8,9},{9,10},{10,1... | collective-permute-start | bytes 98312 | tf_op jit(solution)/shard_map/ppermute | solution.py:22
  13.0 5.3 %copy-start.9 = (f32[16,512]{1,0:T(8,128)}, f32[16,512]{1,0:T(8,128)S(1)}, u32[]{:S(2)}) copy-start(f32[16,512]{1,0:T(8,128)S(1)} %collective-permute-done.refs_1_) | copy-start | bytes 98308
  13.0 24.9 %collective-permute-start.1 = (bf16[3,256,512]{2,1,0:T(8,128)(2,1)S(1)}, bf16[3,256,512]{2,1,0:T(8,128)(2,1)S(1)}, u32[]{:S(2)}, u32[]{:S(2)}) collective-permute-start(bf16[3,256,512]{2,1,0:T(8,128)(2,1)S(1)} %get-tuple-element.26), channel_id=1, source_target_pairs={{0,1},{1,2},{2,3},{3,4},{4,5},{5,6},{6,7},{7,8},{8,9},{9,10},{10,1... | collective-permute-start | bytes 2359304 | tf_op jit(solution)/shard_map/ppermute | solution.py:22
  13.0 24.9 %collective-permute-start.2 = (bf16[3,256,512]{2,1,0:T(8,128)(2,1)S(1)}, bf16[3,256,512]{2,1,0:T(8,128)(2,1)S(1)}, u32[]{:S(2)}, u32[]{:S(2)}) collective-permute-start(bf16[3,256,512]{2,1,0:T(8,128)(2,1)S(1)} %get-tuple-element.27), channel_id=1, source_target_pairs={{0,31},{1,0},{2,1},{3,2},{4,3},{5,4},{6,5},{7,6},{8,7},{9,8},{10,9... | collective-permute-start | bytes 2359304 | tf_op jit(solution)/shard_map/ppermute | solution.py:22
  37.9 0.9 copy-start.2
  37.9 1.2 %copy-start.3 = (bf16[3,256,512]{2,1,0:T(8,128)(2,1)}, bf16[3,256,512]{2,1,0:T(8,128)(2,1)S(1)}, u32[]{:S(2)}) copy-start(bf16[3,256,512]{2,1,0:T(8,128)(2,1)S(1)} %collective-permute-done.2.refs_4_) | copy-start | bytes 2359300
  48.4 1.7 %collective-permute-start.3 = (f32[8,512]{1,0:T(8,128)}, f32[8,512]{1,0:T(8,128)S(1)}, u32[]{:S(2)}, u32[]{:S(2)}) collective-permute-start(f32[8,512]{1,0:T(8,128)} %get-tuple-element.35.refs_5_), channel_id=1, source_target_pairs={{0,31},{1,0},{2,1},{3,2},{4,3},{5,4},{6,5},{7,6},{8,7},{9,8},{10,9... | collective-permute-start | bytes 49160 | tf_op jit(solution)/shard_map/ppermute | solution.py:22
  48.4 7.1 %collective-permute-start.4 = (f32[8,512]{1,0:T(8,128)}, f32[8,512]{1,0:T(8,128)S(1)}, u32[]{:S(2)}, u32[]{:S(2)}) collective-permute-start(f32[8,512]{1,0:T(8,128)} %get-tuple-element.32.refs_2_), channel_id=1, source_target_pairs={{0,1},{1,2},{2,3},{3,4},{4,5},{5,6},{6,7},{7,8},{8,9},{9,10},{10,1... | collective-permute-start | bytes 49160 | tf_op jit(solution)/shard_map/ppermute | solution.py:22
  50.1 10.8 %copy-start.7 = (f32[8,512]{1,0:T(8,128)}, f32[8,512]{1,0:T(8,128)S(1)}, u32[]{:S(2)}) copy-start(f32[8,512]{1,0:T(8,128)S(1)} %collective-permute-done.3.refs_3_) | copy-start | bytes 49156
  55.5 5.3 %copy-start.10 = (f32[8,512]{1,0:T(8,128)}, f32[8,512]{1,0:T(8,128)S(1)}, u32[]{:S(2)}) copy-start(f32[8,512]{1,0:T(8,128)S(1)} %collective-permute-done.4.refs_4_) | copy-start | bytes 49156
  55.5 24.9 %collective-permute-start.5 = (bf16[3,256,512]{2,1,0:T(8,128)(2,1)}, bf16[3,256,512]{2,1,0:T(8,128)(2,1)S(1)}, u32[]{:S(2)}, u32[]{:S(2)}) collective-permute-start(bf16[3,256,512]{2,1,0:T(8,128)(2,1)} %get-tuple-element.39), channel_id=1, source_target_pairs={{0,1},{1,2},{2,3},{3,4},{4,5},{5,6},{6,7},{7,8},{8,9},{9,10},{10,1... | collective-permute-start | bytes 2359304 | tf_op jit(solution)/shard_map/ppermute | solution.py:22
  55.5 24.9 %collective-permute-start.6 = (bf16[3,256,512]{2,1,0:T(8,128)(2,1)}, bf16[3,256,512]{2,1,0:T(8,128)(2,1)S(1)}, u32[]{:S(2)}, u32[]{:S(2)}) collective-permute-start(bf16[3,256,512]{2,1,0:T(8,128)(2,1)} %get-tuple-element.40), channel_id=1, source_target_pairs={{0,31},{1,0},{2,1},{3,2},{4,3},{5,4},{6,5},{7,6},{8,7},{9,8},{10,9... | collective-permute-start | bytes 2359304 | tf_op jit(solution)/shard_map/ppermute | solution.py:22
  80.5 0.9 copy-start
  80.5 1.1 %copy-start.1 = (bf16[3,256,512]{2,1,0:T(8,128)(2,1)}, bf16[3,256,512]{2,1,0:T(8,128)(2,1)S(1)}, u32[]{:S(2)}) copy-start(bf16[3,256,512]{2,1,0:T(8,128)(2,1)S(1)} %collective-permute-done.6.refs_4_) | copy-start | bytes 2359300
  81.6 11.0 %copy-start.4 = (f32[3,512]{1,0:T(4,128)S(1)}, f32[3,512]{1,0:T(4,128)}, u32[]{:S(2)}) copy-start(f32[3,512]{1,0:T(4,128)} %param.7) | copy-start | bytes 18436
  81.6 11.0 %copy-start.6 = (f32[8,512]{1,0:T(8,128)S(1)}, f32[8,512]{1,0:T(8,128)}, u32[]{:S(2)}) copy-start(f32[8,512]{1,0:T(8,128)} %get-tuple-element.32.refs_2_) | copy-start | bytes 49156
  81.6 11.0 %copy-start.8 = (f32[8,512]{1,0:T(8,128)S(1)}, f32[8,512]{1,0:T(8,128)}, u32[]{:S(2)}) copy-start(f32[8,512]{1,0:T(8,128)} %copy-done.7) | copy-start | bytes 49156
  90.9 1.7 %collective-permute-start.7 = (f32[8,512]{1,0:T(8,128)}, f32[8,512]{1,0:T(8,128)S(1)}, u32[]{:S(2)}, u32[]{:S(2)}) collective-permute-start(f32[8,512]{1,0:T(8,128)} %get-tuple-element.43), channel_id=1, source_target_pairs={{0,31},{1,0},{2,1},{3,2},{4,3},{5,4},{6,5},{7,6},{8,7},{9,8},{10,9... | collective-permute-start | bytes 49160 | tf_op jit(solution)/shard_map/ppermute | solution.py:22

commit v2 on v1

--- a/solution.py
+++ b/solution.py
@@ -83,47 +83,23 @@
     lax.fori_loop(0, table_ref.shape[0] // chunk, body, 0)
 
 
-def spread_kernel(layers, n_moved, *refs):
-    own_ref, near_ref = refs[:2]
-    moved = refs[2 : 2 + n_moved]
-    v_hbm, p_hbm, col = refs[2 + n_moved : 5 + n_moved]
-    vbuf, obuf, force, lhs, xtab, ytab, rowg, in_sem, out_sem = refs[5 + n_moved :]
-    ny, nx = vbuf.shape[2], vbuf.shape[3]
-    both = xtab.shape[0]
-
-    load = pltpu.make_async_copy(v_hbm, vbuf, in_sem)
-    load.start()
-
-    offsets, cells, level, forces = joined(own_ref, near_ref, moved, layers)
-    weights = weights_of(offsets)
-    planes = plane_weights(level, [w[2:3] for w in weights], layers)
-    rows = []
-    for a in range(2):
-        rows += [cells[a : a + 1].astype(jnp.float32)] + [w[a : a + 1] for w in weights]
-    col[...] = columns_of(rows + planes)
+def stencil_kernel(v_hbm, p_hbm, vbuf, obuf, in_sem, out_sem):
+    layers, ny, nx = vbuf.shape[1:]
+
+    def load(z):
+        return pltpu.make_async_copy(v_hbm.at[:, z], vbuf.at[:, z], in_sem.at[z])
+
+    def store(z):
+        return pltpu.make_async_copy(obuf.at[:, z], p_hbm.at[:, z], out_sem.at[z])
+
     for z in range(layers):
-        rowg[z] = jnp.concatenate([forces * planes[z], jnp.zeros((5, both), jnp.float32)], axis=0)
-    fill_xtable(xtab, col, 0, jnp.bfloat16, nx, TABLE)
-
-    wy = [w[1:2] for w in weights]
-
-    def ybody(i, _):
-        across = lax.broadcasted_iota(jnp.int32, (32, both), 0) + i * 32
-        ytab[pl.ds(i * 32, 32), :] = banded(across, cells[1:2], wy, ny)
-        return 0
-
-    lax.fori_loop(0, ny // 32, ybody, 0)
-    load.wait()
+        load(z).start()
+    load(0).wait()
 
     def plane(z, _):
-        def lhs_body(i, _):
-            y = ytab[pl.ds(i * 16, 16), :]
-            for c in range(3):
-                lhs[pl.ds(c * ny + i * 16, 16), :] = (rowg[z, c : c + 1, :] * y).astype(jnp.bfloat16)
-            return 0
-
-        lax.fori_loop(0, ny // 16, lhs_body, 0)
-        force[...] = jnp.dot(lhs[...], xtab[...], preferred_element_type=jnp.float32)
+        @pl.when(z < layers - 1)
+        def _():
+            load(z + 1).wait()
 
         below = jnp.maximum(z - 1, 0)
         above = jnp.minimum(z + 1, layers - 1)
@@ -131,7 +107,7 @@
         has_above = jnp.where(z < layers - 1, 1.0, 0.0)
 
         def stencil(i, _):
-            n = 16
+            n = 8
             y0 = i * n
             prev = jnp.where(i == 0, ny - 8, y0 - 8)
             nxt = jnp.where(y0 + n == ny, 0, y0 + n)
@@ -144,7 +120,7 @@
                 window = jnp.concatenate(
                     [vbuf[c, z, pl.ds(prev, 8), :], here[c], vbuf[c, z, pl.ds(nxt, 8), :]], axis=0
                 )
-                total = (1.0 - 6.0 * DT * VISC) * here[c] + DT * force[pl.ds(c * ny + y0, n), :]
+                total = (1.0 - 6.0 * DT * VISC) * here[c]
                 total += up[0] * pltpu.roll(here[c], nx - 1, 1) + down[0] * pltpu.roll(here[c], 1, 1)
                 total += up[1] * pltpu.roll(window, n + 15, 0)[8 : 8 + n]
                 total += down[1] * pltpu.roll(window, 1, 0)[8 : 8 + n]
@@ -153,7 +129,85 @@
                 obuf[c, z, pl.ds(y0, n), :] = total
             return 0
 
-        lax.fori_loop(0, ny // 16, stencil, 0)
+        lax.fori_loop(0, ny // 8, stencil, 0, unroll=2)
+        store(z).start()
+        return 0
+
+    lax.fori_loop(0, layers, plane, 0)
+    for z in range(layers):
+        store(z).wait()
+
+
+def stencil_terms(velocity):
+    layers = velocity.shape[1]
+    hbm = pl.BlockSpec(memory_space=pl.ANY)
+    return pl.pallas_call(
+        stencil_kernel,
+        out_shape=jax.ShapeDtypeStruct(velocity.shape, jnp.float32),
+        in_specs=[hbm],
+        out_specs=hbm,
+        scratch_shapes=[
+            pltpu.VMEM(velocity.shape, jnp.float32),
+            pltpu.VMEM(velocity.shape, jnp.float32),
+            pltpu.SemaphoreType.DMA((layers,)),
+            pltpu.SemaphoreType.DMA((layers,)),
+        ],
+        cost_estimate=pl.CostEstimate(
+            flops=6000 * velocity.size, bytes_accessed=8 * velocity.size, transcendentals=0
+        ),
+        name="stencil_terms",
+    )(velocity)
+
+
+def spread_kernel(layers, n_moved, *refs):
+    own_ref, near_ref = refs[:2]
+    moved = refs[2 : 2 + n_moved]
+    v_hbm, p_hbm, col = refs[2 + n_moved : 5 + n_moved]
+    obuf, force, lhs, xtab, ytab, rowg, in_sem, out_sem = refs[5 + n_moved :]
+    ny, nx = obuf.shape[2], obuf.shape[3]
+    both = xtab.shape[0]
+
+    load = pltpu.make_async_copy(v_hbm, obuf, in_sem)
+    load.start()
+
+    offsets, cells, level, forces = joined(own_ref, near_ref, moved, layers)
+    weights = weights_of(offsets)
+    planes = plane_weights(level, [w[2:3] for w in weights], layers)
+    rows = []
+    for a in range(2):
+        rows += [cells[a : a + 1].astype(jnp.float32)] + [w[a : a + 1] for w in weights]
+    col[...] = columns_of(rows + planes)
+    for z in range(layers):
+        rowg[z] = jnp.concatenate([forces * planes[z], jnp.zeros((5, both), jnp.float32)], axis=0)
+    fill_xtable(xtab, col, 0, jnp.bfloat16, nx, TABLE)
+
+    wy = [w[1:2] for w in weights]
+
+    def ybody(i, _):
+        across = lax.broadcasted_iota(jnp.int32, (32, both), 0) + i * 32
+        ytab[pl.ds(i * 32, 32), :] = banded(across, cells[1:2], wy, ny)
+        return 0
+
+    lax.fori_loop(0, ny // 32, ybody, 0)
+    load.wait()
+
+    def plane(z, _):
+        def lhs_body(i, _):
+            y = ytab[pl.ds(i * 16, 16), :]
+            for c in range(3):
+                lhs[pl.ds(c * ny + i * 16, 16), :] = (rowg[z, c : c + 1, :] * y).astype(jnp.bfloat16)
+            return 0
+
+        lax.fori_loop(0, ny // 16, lhs_body, 0)
+        force[...] = jnp.dot(lhs[...], xtab[...], preferred_element_type=jnp.float32)
+
+        def add(i, _):
+            r = pl.ds(i * 32, 32)
+            for c in range(3):
+                obuf[c, z, r, :] += DT * force[pl.ds(c * ny + i * 32, 32), :]
+            return 0
+
+        lax.fori_loop(0, ny // 32, add, 0)
         pltpu.make_async_copy(obuf.at[:, z], p_hbm.at[:, z], out_sem.at[z]).start()
         return 0
 
@@ -162,7 +216,7 @@
         pltpu.make_async_copy(obuf.at[:, z], p_hbm.at[:, z], out_sem.at[z]).wait()
 
 
-def spread_and_advance(own, near, moved, velocity):
+def add_forcing(own, near, moved, velocity):
     _, layers, ny, nx = velocity.shape
     both = 2 * own.shape[1]
     vmem = pl.BlockSpec(memory_space=pltpu.VMEM)
@@ -176,8 +230,8 @@
         ],
         in_specs=[vmem] * (2 + len(moved)) + [hbm],
         out_specs=[hbm, vmem],
+        input_output_aliases={2 + len(moved): 0},
         scratch_shapes=[
-            pltpu.VMEM(velocity.shape, jnp.float32),
             pltpu.VMEM(velocity.shape, jnp.float32),
             pltpu.VMEM((3 * ny, nx), jnp.float32),
             pltpu.VMEM((3 * ny, both), jnp.bfloat16),
@@ -190,7 +244,7 @@
         cost_estimate=pl.CostEstimate(
             flops=flops, bytes_accessed=8 * velocity.size, transcendentals=0
         ),
-        name="spread_and_advance",
+        name="add_forcing",
     )(own, near, *moved, velocity)
 
 
@@ -327,17 +381,15 @@
     )
     first = velocity[:, 0].astype(jnp.bfloat16)
     final = velocity[:, layers - 1].astype(jnp.bfloat16)
+    own, first, final = lax.optimization_barrier((own, first, final))
     near = shifted(own, 1)
     moved = ()
     for step in range(STEPS):
         last = step == STEPS - 1
-        if moved:
-            first, final, *moved = lax.optimization_barrier((first, final, *moved))
-        else:
-            first, final, near = lax.optimization_barrier((first, final, near))
         before = shifted(final, 1)
         after = shifted(first, -1)
-        partial, col = spread_and_advance(own, near, moved, velocity)
+        partial = stencil_terms(velocity)
+        partial, col = add_forcing(own, near, moved, partial)
         velocity, own_part, near_part, *low = finish_and_sample(
             col, velocity, partial, before, after, 0 if last else 1
         )

time: 94.7 us -> 92.7 us (0.979)
  waiting for transfers between devices: 13.7 us -> 1.67 us
  Pallas kernels: 57.6 us -> 64.5 us
  local copies, waits for them, and re-layouts: 5.98 us -> 7.74 us
  starting transfers between devices: 11.8 us -> 13.2 us
    ppermute x8, waiting for transfers between devices: 13.7 us -> 1.67 us  [shifted(): return lax.ppermute(value, 'gz', pairs)]
    pallas_call x2 -> x4, Pallas kernels: 39.1 us -> 46 us  [the longest x2 23.5 us: add_forcing(): pl.pallas_call(functools.partial(spread_kernel, layers, len(moved)), out_...]
    unnamed x22, local copies, waits for them, and re-layouts: 2.35 us -> 4.1 us
    ppermute x8, starting transfers between devices: 11.8 us -> 13.2 us  [shifted(): return lax.ppermute(value, 'gz', pairs)]
  transfers between devices with their start and end apart: 8 -> 8, of which waited for: 4 -> 1; matrix products, arithmetic and copies ran while one was open for 2% -> 0% of each run, Pallas kernels for 42% -> 50%
where the time goes in v2:
time: 92.7 us; the launch traced here: 92 us
  Pallas kernels  64.5 us (70%)
  starting transfers between devices  13.2 us (14%)
  local copies, waits for them, and re-layouts  7.74 us (8%)
  other arithmetic  3.43 us (4%)
  waiting for transfers between devices  1.67 us (2%)
  between operations  1.47 us (2%)
    pallas_call x2, Pallas kernels, add_forcing(): pl.pallas_call(functools.partial(spread_kernel, layers, len(moved)), out_...  23.5 us
    pallas_call x2, Pallas kernels, stencil_terms(): pl.pallas_call(stencil_kernel, out_shape=jax.ShapeDtypeStruct(velocity.sh...  22.5 us
    pallas_call x2, Pallas kernels, finish_and_sample(): pl.pallas_call(functools.partial(sample_kernel, layers, send), out_shape=...  18.5 us
    ppermute x8, starting transfers between devices, shifted(): return lax.ppermute(value, 'gz', pairs)  13.2 us
    unnamed x22, local copies, waits for them, and re-layouts  4.1 us
    convert_element_type x1, local copies, waits for them, and re-layouts, local(): final = velocity[:, layers - 1].astype(jnp.bfloat16)  2.08 us
  transfers between devices with their start and end apart: 8, of which 1 were waited for; matrix products, arithmetic and copies ran while one was open for 0% of the time, Pallas kernels for 50%

profile of v2, /device:TPU:0, one launch (start us, length us, event | category | flops | bytes accessed | tf_op | source)
XLA Modules:
  0.0 92.0 jit_solution(8760859931479075267)
XLA Ops:
  1.3 0.7 slice_convert_fusion
  2.0 0.7 subtract_convert_fusion
  2.7 2.1 %slice_bitcast_fusion = (bf16[3,256,512]{2,1,0:T(8,128)(2,1)S(1)}, bf16[3,256,512]{2,1,0:T(8,128)(2,1)S(1)}) fusion(f32[3,4,256,512]{3,2,1,0:T(8,128)} %refs_1_.1), kind=kLoop, calls=%fused_computation.1 | loop fusion | bytes 3145728 | tf_op jit(solution)/shard_map/convert_element_type | solution.py:383
  4.8 0.7 broadcast_select_fusion
  5.5 1.5 %concatenate.3.refs_0_ = f32[16,512]{1,0:T(8,128)S(1)} concatenate(f32[3,512]{1,0:T(4,128)} %param.7, f32[2,512]{1,0:T(2,128)S(1)} %slice_convert_fusion, f32[1,512]{1,0:T(1,128)S(1)} %subtract_convert_fusion, f32[3,512]{1,0:T(4,128)} %param.9, f32[1,512]{1,0:T(1,128)S(1)} %compare_convert_fusion, f32[1,512]{1,0:T(1,128)S(1)} %bitcast.9, f32[5,512]{1,0:T(8,128)S(1)} %broadcast_in_dim.5), dimensions={0} | concatenate | bytes 65536 | tf_op jit(solution)/shard_map/concatenate | solution.py:370
  7.0 0.5 collective-permute-start
  7.6 2.6 %collective-permute-start.1 = (bf16[3,256,512]{2,1,0:T(8,128)(2,1)S(1)}, bf16[3,256,512]{2,1,0:T(8,128)(2,1)S(1)}, u32[]{:S(2)}, u32[]{:S(2)}) collective-permute-start(bf16[3,256,512]{2,1,0:T(8,128)(2,1)S(1)} %get-tuple-element.20), channel_id=1, source_target_pairs={{0,1},{1,2},{2,3},{3,4},{4,5},{5,6},{6,7},{7,8},{8,9},{9,10},{10,1... | collective-permute-start | bytes 2359304 | tf_op jit(solution)/shard_map/ppermute | solution.py:22
  10.2 3.5 %collective-permute-start.2 = (bf16[3,256,512]{2,1,0:T(8,128)(2,1)S(1)}, bf16[3,256,512]{2,1,0:T(8,128)(2,1)S(1)}, u32[]{:S(2)}, u32[]{:S(2)}) collective-permute-start(bf16[3,256,512]{2,1,0:T(8,128)(2,1)S(1)} %get-tuple-element.21), channel_id=1, source_target_pairs={{0,31},{1,0},{2,1},{3,2},{4,3},{5,4},{6,5},{7,6},{8,7},{9,8},{10,9... | collective-permute-start | bytes 2359304 | tf_op jit(solution)/shard_map/ppermute | solution.py:22
  13.6 11.2 %stencil_terms.2.refs_2_ = f32[3,4,256,512]{3,2,1,0:T(8,128)} custom-call(f32[3,4,256,512]{3,2,1,0:T(8,128)} %refs_1_.1), custom_call_target="tpu_custom_call" | custom-call | flops 9437184000 | bytes 12582912 | tf_op jit(solution)/shard_map/stencil_terms/pallas_call | solution.py:144
  24.9 0.6 copy-done.9
  25.5 11.7 %add_forcing.2 = (f32[3,4,256,512]{3,2,1,0:T(8,128)}, f32[1024,16]{1,0:T(8,128)}) custom-call(f32[16,512]{1,0:T(8,128)} %copy-done.5, f32[16,512]{1,0:T(8,128)} %copy-done.9, f32[3,4,256,512]{3,2,1,0:T(8,128)} %stencil_terms.2.refs_2_), custom_call_target="tpu_custom_call", output_to_operand_aliasing={{0}: (2, {})} | custom-call | flops 3221225472 | bytes 12582912 | tf_op jit(solution)/shard_map/add_forcing/pallas_call | solution.py:225
  37.3 0.8 copy-done.2
  38.5 9.2 %finish_and_sample.2 = (f32[3,4,256,512]{3,2,1,0:T(8,128)}, f32[8,512]{1,0:T(8,128)}, f32[8,512]{1,0:T(8,128)}, bf16[3,256,512]{2,1,0:T(8,128)(2,1)}, bf16[3,256,512]{2,1,0:T(8,128)(2,1)}) custom-call(f32[1024,16]{1,0:T(8,128)} %get-tuple-element.18.refs_0_, f32[3,4,256,512]{3,2,1,0:T(8,128)} %refs_1_.1, ...), custom_call_target="tpu_custom_call", output_to_operand_aliasing={{0}: (2, {})} | custom-call | flops 3221225472 | bytes 6291456 | tf_op jit(solution)/shard_map/finish_and_sample/pallas_call | solution.py:340
  47.7 0.7 collective-permute-start.3
  48.4 5.4 %collective-permute-start.6 = (bf16[3,256,512]{2,1,0:T(8,128)(2,1)}, bf16[3,256,512]{2,1,0:T(8,128)(2,1)S(1)}, u32[]{:S(2)}, u32[]{:S(2)}) collective-permute-start(bf16[3,256,512]{2,1,0:T(8,128)(2,1)} %get-tuple-element.28), channel_id=1, source_target_pairs={{0,31},{1,0},{2,1},{3,2},{4,3},{5,4},{6,5},{7,6},{8,7},{9,8},{10,9... | collective-permute-start | bytes 2359304 | tf_op jit(solution)/shard_map/ppermute | solution.py:22
  53.8 11.2 %stencil_terms.3.refs_6_ = f32[3,4,256,512]{3,2,1,0:T(8,128)} custom-call(f32[3,4,256,512]{3,2,1,0:T(8,128)} %get-tuple-element.24.v_hbm.refs_1_), custom_call_target="tpu_custom_call" | custom-call | flops 9437184000 | bytes 12582912 | tf_op jit(solution)/shard_map/stencil_terms/pallas_call | solution.py:144
  65.1 0.6 copy-done.7
  65.6 0.6 copy-done.10
  66.2 11.8 %add_forcing.3 = (f32[3,4,256,512]{3,2,1,0:T(8,128)}, f32[1024,16]{1,0:T(8,128)}) custom-call(f32[16,512]{1,0:T(8,128)} %copy-done.5, f32[16,512]{1,0:T(8,128)} %copy-done.9, f32[8,512]{1,0:T(8,128)} %get-tuple-element.22.refs_2_, f32[8,512]{1,0:T(8,128)} %copy-done.7, f32[8,512]{1,0:T(8,128)} %copy-done.10, ...), custom_call_target="tpu_custom_call", output_to_operand_aliasing={{0}: (6, {})} | custom-call | flops 3221225472 | bytes 12582912 | tf_op jit(solution)/shard_map/add_forcing/pallas_call | solution.py:225
  78.1 0.9 copy-done
  79.2 9.3 %finish_and_sample.3 = (f32[3,4,256,512]{3,2,1,0:T(8,128)}, f32[8,512]{1,0:T(8,128)}, f32[8,512]{1,0:T(8,128)}) custom-call(f32[1024,16]{1,0:T(8,128)} %get-tuple-element.25.refs_0_, f32[3,4,256,512]{3,2,1,0:T(8,128)} %get-tuple-element.24.v_hbm.refs_1_, f32[3,4,256,512]{3,2,1,0:T(8,128)} %get-tuple-element.26.refs_2_, ...), custom_call_target="tpu_custom_call", output_to_operand_aliasing={{0}: (2, {})} | custom-call | flops 3221225472 | bytes 6291456 | tf_op jit(solution)/shard_map/finish_and_sample/pallas_call | solution.py:340
  88.5 0.5 collective-permute-start.7
  89.1 1.6 %collective-permute-done.7 = f32[8,512]{1,0:T(8,128)S(1)} collective-permute-done((f32[8,512]{1,0:T(8,128)}, f32[8,512]{1,0:T(8,128)S(1)}, u32[]{:S(2)}, u32[]{:S(2)}) %collective-permute-start.7) | collective-permute-done | bytes 16416 | tf_op jit(solution)/shard_map/ppermute | solution.py:22
  90.7 1.3 %fusion.2 = f32[3,512]{1,0:T(4,128)} fusion(f32[8,512]{1,0:T(8,128)S(1)} %collective-permute-done.7, f32[3,512]{1,0:T(4,128)S(1)} %copy-done.4, f32[8,512]{1,0:T(8,128)S(1)} %copy-done.8, f32[8,512]{1,0:T(8,128)} %get-tuple-element.30, f32[8,512]{1,0:T(8,128)S(1)} %copy-done.6, f32[512]{0:T(512)S(1)} %fusion.10), kind=kLoop, calls=%fused_computation.6 | loop fusion | flops 12288 | bytes 38912 | tf_op jit(solution)/shard_map/add | solution.py:400
  (29 shorter events, 0.7 us)
Async XLA Ops:
  7.0 17.8 %copy-start.5 = (f32[16,512]{1,0:T(8,128)}, f32[16,512]{1,0:T(8,128)S(1)}, u32[]{:S(2)}) copy-start(f32[16,512]{1,0:T(8,128)S(1)} %concatenate.3.refs_0_) | copy-start | bytes 98308
  7.0 17.8 %collective-permute-start = (f32[16,512]{1,0:T(8,128)S(1)}, f32[16,512]{1,0:T(8,128)S(1)}, u32[]{:S(2)}, u32[]{:S(2)}) collective-permute-start(f32[16,512]{1,0:T(8,128)S(1)} %concatenate.3.refs_0_), channel_id=1, source_target_pairs={{0,1},{1,2},{2,3},{3,4},{4,5},{5,6},{6,7},{7,8},{8,9},{9,10},{10,1... | collective-permute-start | bytes 98312 | tf_op jit(solution)/shard_map/ppermute | solution.py:22
  7.6 29.7 %collective-permute-start.1 = (bf16[3,256,512]{2,1,0:T(8,128)(2,1)S(1)}, bf16[3,256,512]{2,1,0:T(8,128)(2,1)S(1)}, u32[]{:S(2)}, u32[]{:S(2)}) collective-permute-start(bf16[3,256,512]{2,1,0:T(8,128)(2,1)S(1)} %get-tuple-element.20), channel_id=1, source_target_pairs={{0,1},{1,2},{2,3},{3,4},{4,5},{5,6},{6,7},{7,8},{8,9},{9,10},{10,1... | collective-permute-start | bytes 2359304 | tf_op jit(solution)/shard_map/ppermute | solution.py:22
  10.2 27.1 %collective-permute-start.2 = (bf16[3,256,512]{2,1,0:T(8,128)(2,1)S(1)}, bf16[3,256,512]{2,1,0:T(8,128)(2,1)S(1)}, u32[]{:S(2)}, u32[]{:S(2)}) collective-permute-start(bf16[3,256,512]{2,1,0:T(8,128)(2,1)S(1)} %get-tuple-element.21), channel_id=1, source_target_pairs={{0,31},{1,0},{2,1},{3,2},{4,3},{5,4},{6,5},{7,6},{8,7},{9,8},{10,9... | collective-permute-start | bytes 2359304 | tf_op jit(solution)/shard_map/ppermute | solution.py:22
  24.9 0.6 copy-start.9
  37.2 0.9 copy-start.2
  37.3 1.2 %copy-start.3 = (bf16[3,256,512]{2,1,0:T(8,128)(2,1)}, bf16[3,256,512]{2,1,0:T(8,128)(2,1)S(1)}, u32[]{:S(2)}) copy-start(bf16[3,256,512]{2,1,0:T(8,128)(2,1)S(1)} %collective-permute-done.2.refs_4_) | copy-start | bytes 2359300
  47.7 17.3 %collective-permute-start.3 = (f32[8,512]{1,0:T(8,128)}, f32[8,512]{1,0:T(8,128)S(1)}, u32[]{:S(2)}, u32[]{:S(2)}) collective-permute-start(f32[8,512]{1,0:T(8,128)} %get-tuple-element.23.refs_5_), channel_id=1, source_target_pairs={{0,31},{1,0},{2,1},{3,2},{4,3},{5,4},{6,5},{7,6},{8,7},{9,8},{10,9... | collective-permute-start | bytes 49160 | tf_op jit(solution)/shard_map/ppermute | solution.py:22
  48.4 16.6 %collective-permute-start.4 = (f32[8,512]{1,0:T(8,128)}, f32[8,512]{1,0:T(8,128)S(1)}, u32[]{:S(2)}, u32[]{:S(2)}) collective-permute-start(f32[8,512]{1,0:T(8,128)} %get-tuple-element.22.refs_2_), channel_id=1, source_target_pairs={{0,1},{1,2},{2,3},{3,4},{4,5},{5,6},{6,7},{7,8},{8,9},{9,10},{10,1... | collective-permute-start | bytes 49160 | tf_op jit(solution)/shard_map/ppermute | solution.py:22
  48.4 29.6 %collective-permute-start.5 = (bf16[3,256,512]{2,1,0:T(8,128)(2,1)}, bf16[3,256,512]{2,1,0:T(8,128)(2,1)S(1)}, u32[]{:S(2)}, u32[]{:S(2)}) collective-permute-start(bf16[3,256,512]{2,1,0:T(8,128)(2,1)} %get-tuple-element.27), channel_id=1, source_target_pairs={{0,1},{1,2},{2,3},{3,4},{4,5},{5,6},{6,7},{7,8},{8,9},{9,10},{10,1... | collective-permute-start | bytes 2359304 | tf_op jit(solution)/shard_map/ppermute | solution.py:22
  48.4 29.6 %collective-permute-start.6 = (bf16[3,256,512]{2,1,0:T(8,128)(2,1)}, bf16[3,256,512]{2,1,0:T(8,128)(2,1)S(1)}, u32[]{:S(2)}, u32[]{:S(2)}) collective-permute-start(bf16[3,256,512]{2,1,0:T(8,128)(2,1)} %get-tuple-element.28), channel_id=1, source_target_pairs={{0,31},{1,0},{2,1},{3,2},{4,3},{5,4},{6,5},{7,6},{8,7},{9,8},{10,9... | collective-permute-start | bytes 2359304 | tf_op jit(solution)/shard_map/ppermute | solution.py:22
  65.0 0.6 copy-start.7
  65.6 0.6 copy-start.10
  78.0 0.9 copy-start
  78.1 1.1 %copy-start.1 = (bf16[3,256,512]{2,1,0:T(8,128)(2,1)}, bf16[3,256,512]{2,1,0:T(8,128)(2,1)S(1)}, u32[]{:S(2)}) copy-start(bf16[3,256,512]{2,1,0:T(8,128)(2,1)S(1)} %collective-permute-done.6.refs_4_) | copy-start | bytes 2359300
  79.2 11.5 %copy-start.4 = (f32[3,512]{1,0:T(4,128)S(1)}, f32[3,512]{1,0:T(4,128)}, u32[]{:S(2)}) copy-start(f32[3,512]{1,0:T(4,128)} %param.7) | copy-start | bytes 18436
  79.2 11.5 %copy-start.6 = (f32[8,512]{1,0:T(8,128)S(1)}, f32[8,512]{1,0:T(8,128)}, u32[]{:S(2)}) copy-start(f32[8,512]{1,0:T(8,128)} %get-tuple-element.22.refs_2_) | copy-start | bytes 49156
  79.2 11.5 %copy-start.8 = (f32[8,512]{1,0:T(8,128)S(1)}, f32[8,512]{1,0:T(8,128)}, u32[]{:S(2)}) copy-start(f32[8,512]{1,0:T(8,128)} %copy-done.7) | copy-start | bytes 49156
  88.5 2.2 %collective-permute-start.7 = (f32[8,512]{1,0:T(8,128)}, f32[8,512]{1,0:T(8,128)S(1)}, u32[]{:S(2)}, u32[]{:S(2)}) collective-permute-start(f32[8,512]{1,0:T(8,128)} %get-tuple-element.31), channel_id=1, source_target_pairs={{0,31},{1,0},{2,1},{3,2},{4,3},{5,4},{6,5},{7,6},{8,7},{9,8},{10,9... | collective-permute-start | bytes 49160 | tf_op jit(solution)/shard_map/ppermute | solution.py:22
